TPU v7x, 256 devices: a whole 4x4x8 slice. The times are simulated.
256 devices in a mesh: seq: 32 (over x, z), batch: 8 (over y, core).
Axes of the slice: x: 4, y: 4, z: 8, core: 2. Of those that a mesh axis runs over, the one named last changes fastest.
Arguments:
- hidden: bfloat16 [16, 8192, 4096], P('batch', None, 'seq')
- gain: float32 [4096], P('seq'), may hold values from 0.5 to 1.5
- value_weight: float32 [4096], P('seq'), may hold values from -0.09375 to 0.09375
- rewards: float32 [16, 8192], P('batch', 'seq'), may hold values from -1.5 to 1.5
- reward_mask: int32 [16, 8192], P('batch', 'seq'), may hold values 0 or 1
- lengths: int32 [16], P('batch'), may hold values from 2048 to 8192
- horizon: float32 [16], P('batch'), may hold values from 24 to 65536
Outputs:
- advantages: float32 [16, 8192], P(None, ('seq', 'batch'))
- returns: float32 [16, 8192], P(None, ('seq', 'batch'))
All inputs are finite; a program needn't handle non-finite values. No bound on the sum of `reward_mask` on one device may be relied on, other than what follows from the above.
Results may differ from a plain program's by a relative error of at most 0.0003.
Values may be sent and summed in bfloat16 or wider, within the bound.
A program may use at most 64 MiB of HBM per device.

v0:
```python
import jax
import jax.numpy as jnp
from jax import lax
from jax.sharding import Mesh
from jax.sharding import PartitionSpec as P

D = 4096
SEQ = ("seq_0", "seq_1")
SEQ_BATCH = ("seq_0", "seq_1", "batch_0", "batch_1")
BATCH = ("batch_0", "batch_1")
EPS = 1e-05


def cut_along(array, dim, devices):
    dims = array.shape
    blocks = array.reshape(*dims[:dim], devices, dims[dim] // devices, *dims[dim + 1 :])
    return jnp.moveaxis(blocks, dim, 0)


def sent_and_summed(array, axis, dim):
    devices = lax.axis_size(axis)
    blocks = lax.all_to_all(cut_along(array, dim, devices), axis, 0, 0, tiled=True)
    return jnp.sum(blocks, axis=0)


def side_by_side(arrays, axis, dim, along):
    widths = [a.shape[along] for a in arrays]
    both = jnp.concatenate(arrays, axis=along)
    whole = sent_and_summed(both, axis, dim)
    return tuple(jnp.split(whole, [sum(widths[:k]) for k in range(1, len(widths))], axis=along))


def from_behind(value, axis, steps):
    count = lax.axis_size(axis)
    initial, last = (max(0, -steps), min(count, count - steps))
    return lax.ppermute(value, axis, [(source, source + steps) for source in range(initial, last)])


def sent_to_all(array, axis):
    devices = lax.axis_size(axis)
    return lax.all_to_all(
        jnp.broadcast_to(array[None], (devices, *array.shape)), axis, 0, 0, tiled=True
    )


def gathered_once(array, axis):
    leaves = jax.tree.leaves(array)
    turns = sorted(range(len(leaves)), key=lambda k: -leaves[k].size)
    width = (1, *leaves[turns[0]].shape)[-1]
    lines = [
        jnp.pad(leaves[k].reshape(-1), (0, -leaves[k].size % width)).reshape(-1, width)
        for k in turns
    ]
    both, at, found = (sent_to_all(jnp.concatenate(lines), axis), 0, {})
    for k, line in zip(turns, lines):
        slab = both[:, at : at + len(line)].reshape(len(both), -1)
        found[k] = slab[:, : leaves[k].size].reshape(-1, *leaves[k].shape)
        at += len(line)
    numbers = iter(range(len(leaves)))
    return jax.tree.map(lambda _: found[next(numbers)], array)


def joined_by_halves(pieces, combine):
    while len(jax.tree.leaves(pieces)[0]) > 1:
        pieces = jax.vmap(combine)(
            *(jax.tree.map(lambda part: part[side::2], pieces) for side in (0, 1))
        )
    return jax.tree.map(lambda part: part[0], pieces)


def prefix(array, axis, combine, identity):
    devices, position = (lax.axis_size(axis), lax.axis_index(axis))
    passed = jnp.arange(devices) > position

    def kept(part, zero, own):
        part = jnp.where(
            passed.reshape(-1, *(1 for _ in own.shape)), part, jnp.asarray(zero, own.dtype)
        )
        return part[::-1]

    pieces = gathered_once(array, axis)
    return joined_by_halves(jax.tree.map(kept, pieces, identity, array), combine)


def one_axis_at_a_time(array, axes):
    for axis in axes:
        array = lax.psum(array, axis)
    return array


def per_device(hidden, gain, value_weight, rewards, reward_mask, lengths, horizon):
    my_index = lax.axis_index(SEQ)
    block = rewards.shape[1]
    wide_rows = hidden.astype(jnp.float32)
    part_squares = jnp.sum(wide_rows * wide_rows, -1)
    part_projected = jnp.sum(wide_rows * (gain * value_weight), -1)
    squares, projected = side_by_side((part_squares, part_projected), SEQ, 1, 0)
    values = projected * lax.rsqrt(squares / D + EPS)
    positions = my_index * block + jnp.arange(block, dtype=jnp.int32)
    valid = (positions[None, :] < lengths[:, None]).astype(jnp.float32)
    next_valid = (positions[None, :] + 1 < lengths[:, None]).astype(jnp.float32)
    following = from_behind(values[:, 0], SEQ, -1)
    next_values = jnp.concatenate([values[:, 1:], following[:, None]], 1)
    delta = (rewards * reward_mask.astype(jnp.float32) + next_valid * next_values - values) * valid
    log_decay = -1.0 / horizon
    offsets = jnp.arange(block, dtype=jnp.int32)
    distance = (offsets[None, :] - offsets[:, None]).astype(jnp.float32)
    upper_mask = distance >= 0.0
    powers = jnp.where(
        upper_mask[None], jnp.exp(jnp.maximum(distance, 0.0)[None] * log_decay[:, None, None]), 0.0
    )
    local_gae = jnp.einsum("rtk,rk->rt", powers, delta, precision=lax.Precision.HIGHEST)
    tail_decay = jnp.exp((block - offsets).astype(jnp.float32)[None, :] * log_decay[:, None])
    start_value = local_gae[:, 0]
    block_decay = jnp.exp(block * log_decay)

    def compose(earlier, later):
        return (later[0] + later[1] * earlier[0], later[1] * earlier[1])

    carry_in, _ = prefix(
        (start_value, block_decay),
        SEQ,
        compose,
        (jnp.zeros_like(start_value), jnp.ones_like(block_decay)),
    )
    gae = local_gae + tail_decay * carry_in[:, None]
    returns = (gae + values) * valid
    count, first, second = (
        one_axis_at_a_time(jnp.sum(valid), SEQ_BATCH),
        one_axis_at_a_time(jnp.sum(gae), SEQ_BATCH),
        one_axis_at_a_time(jnp.sum(gae * gae), SEQ_BATCH),
    )
    mean = first / count
    var = jnp.maximum(second / count - mean * mean, 1.0)
    whitened = (gae - mean) * valid * lax.rsqrt(var)
    out_adv, out_returns = (
        lax.all_to_all(whitened, BATCH, split_axis=1, concat_axis=0, tiled=True),
        lax.all_to_all(returns, BATCH, split_axis=1, concat_axis=0, tiled=True),
    )
    return (out_adv, out_returns)


def solution(mesh):
    finer = Mesh(mesh.devices.reshape(4, 8, 4, 2), ("seq_0", "seq_1", "batch_0", "batch_1"))
    placed = (P(BATCH, None, SEQ), P(SEQ), P(SEQ), P(BATCH, SEQ), P(BATCH, SEQ), P(BATCH), P(BATCH))
    return jax.shard_map(
        per_device,
        mesh=finer,
        in_specs=placed,
        out_specs=(P(None, SEQ_BATCH), P(None, SEQ_BATCH)),
        check_vma=False,
    )
```

profile of v0, /device:TPU:1, one launch (start us, length us, event | category | flops | bytes accessed | tf_op | source)
XLA Modules:
  0.0 118.5 jit_solution(17248735630217335933)
XLA Ops:
  0.7 0.7 mul.124
  1.4 6.7 %fusion = (f32[2,8192]{1,0:T(2,128)S(1)}, f32[2,8192]{1,0:T(2,128)S(1)}) fusion(bf16[2,8192,128]{2,1,0:T(8,128)(2,1)} %param.7, f32[128]{0:T(128)S(1)} %mul.124), kind=kLoop, calls=%fused_computation.2 | loop fusion | flops 10452992 | bytes 4325888 | tf_op jit(solution)/shard_map/reduce_sum | solution.py:95
  8.0 0.7 pad_maximum_fusion
  8.7 11.9 %all-to-all-start = ((f32[32,4,256]{2,1,0:T(4,128)}), f32[32,4,256]{2,1,0:T(4,128)S(1)}, u32[]{:S(2)}, u32[]{:S(2)}) async-start(f32[32,4,256]{2,1,0:T(4,128)} %bitcast.1), calls=%async_computation | async-start | bytes 262144 | tf_op jit(solution)/shard_map/all_to_all | solution.py:22
  20.8 9.0 %all-to-all-done = f32[32,4,256]{2,1,0:T(4,128)S(1)} async-done(((f32[32,4,256]{2,1,0:T(4,128)}), f32[32,4,256]{2,1,0:T(4,128)S(1)}, u32[]{:S(2)}, u32[]{:S(2)}) %all-to-all-start) | async-done | bytes 131104 | tf_op jit(solution)/shard_map/all_to_all | solution.py:22
  30.0 1.3 %collective-permute-start = (f32[2]{0:T(128)S(1)}, f32[2]{0:T(128)S(1)}, u32[]{:S(2)}, u32[]{:S(2)}) collective-permute-start(f32[2]{0:T(128)S(1)} %slice_reduce_fusion.1), channel_id=1, source_target_pairs={{8,0},{16,8},{24,16},{32,24},{40,32},{48,40},{56,48},{64,56},{72,6... | collective-permute-start | bytes 32 | tf_op jit(solution)/shard_map/ppermute | solution.py:36
  31.3 3.0 %collective-permute-done = f32[2]{0:T(128)S(1)} collective-permute-done((f32[2]{0:T(128)S(1)}, f32[2]{0:T(128)S(1)}, u32[]{:S(2)}, u32[]{:S(2)}) %collective-permute-start) | collective-permute-done | bytes 40 | tf_op jit(solution)/shard_map/ppermute | solution.py:36
  34.5 0.7 fusion.2
  35.3 0.6 broadcast_in_dim.55
  35.9 5.2 %all-to-all-start.1 = ((f32[32,2,2]{2,1,0:T(2,128)}), f32[32,2,2]{2,1,0:T(2,128)S(1)}, u32[]{:S(2)}, u32[]{:S(2)}) async-start(f32[32,2,2]{2,1,0:T(2,128)} %broadcast_in_dim.55), calls=%async_computation.1 | async-start | bytes 65536 | tf_op jit(solution)/shard_map/all_to_all | solution.py:41
  41.1 8.8 %all-to-all-done.1 = f32[32,2,2]{2,1,0:T(2,128)S(1)} async-done(((f32[32,2,2]{2,1,0:T(2,128)}), f32[32,2,2]{2,1,0:T(2,128)S(1)}, u32[]{:S(2)}, u32[]{:S(2)}) %all-to-all-start.1) | async-done | bytes 544 | tf_op jit(solution)/shard_map/all_to_all | solution.py:41
  52.3 0.7 compare_select_fusion
  53.0 0.6 fusion.20
  53.6 7.6 %all-reduce.2 = (f32[]{:T(128)}, f32[]{:T(128)}, f32[]{:T(128)}) all-reduce(f32[]{:T(128)} %get-tuple-element.5, f32[]{:T(128)} %get-tuple-element.24, f32[]{:T(128)} %get-tuple-element.4), channel_id=1, replica_groups=mesh['seq_0'=4,'seq_1'=8,'batch_0'=4,'batch_1'=2] {'seq_0'}, use_global_device_ids=true, to_apply=%region_14.15 | all-reduce | flops 3 | bytes 24 | tf_op jit(solution)/shard_map/psum | solution.py:87
  61.1 11.8 %all-reduce = (f32[]{:T(128)}, f32[]{:T(128)}, f32[]{:T(128)}) all-reduce(f32[]{:T(128)} %get-tuple-element.12, f32[]{:T(128)} %get-tuple-element.13, f32[]{:T(128)} %get-tuple-element.14), channel_id=1, replica_groups=mesh['seq_0'=4,'seq_1'=8,'batch_0'=4,'batch_1'=2] {'seq_1'}, use_global_device_ids=true, to_apply=%region_15.16 | all-reduce | flops 3 | bytes 24 | tf_op jit(solution)/shard_map/psum | solution.py:87
  72.9 9.7 %all-reduce.1 = (f32[]{:T(128)}, f32[]{:T(128)}, f32[]{:T(128)}) all-reduce(f32[]{:T(128)} %get-tuple-element.6, f32[]{:T(128)} %get-tuple-element.7, f32[]{:T(128)} %get-tuple-element.8), channel_id=1, replica_groups=mesh['seq_0'=4,'seq_1'=8,'batch_0'=4,'batch_1'=2] {'batch_0'}, use_global_device_ids=true, to_apply=%region_16.17 | all-reduce | flops 3 | bytes 24 | tf_op jit(solution)/shard_map/psum | solution.py:87
  82.6 14.5 %all-reduce.3 = (f32[]{:T(128)}, f32[]{:T(128)}, f32[]{:T(128)}) all-reduce(f32[]{:T(128)} %get-tuple-element.9, f32[]{:T(128)} %get-tuple-element.10, f32[]{:T(128)} %get-tuple-element.11), channel_id=1, replica_groups=mesh['seq_0'=4,'seq_1'=8,'batch_0'=4,'batch_1'=2] {'batch_1'}, use_global_device_ids=true, to_apply=%region_17.18 | all-reduce | flops 3 | bytes 24 | tf_op jit(solution)/shard_map/psum | solution.py:87
  99.9 0.6 copy.18
  100.6 3.6 %all-to-all-start.2 = ((f32[2,8,32]{2,0,1:T(2,128)}), f32[2,8,32]{2,0,1:T(2,128)S(1)}, u32[]{:S(2)}, u32[]{:S(2)}) async-start(f32[2,8,32]{2,0,1:T(2,128)} %copy.18), calls=%async_computation.2 | async-start | bytes 16384 | tf_op jit(solution)/shard_map/all_to_all | solution.py:137
  104.2 0.6 copy.19
  104.8 4.0 %all-to-all-done.2 = f32[2,8,32]{2,0,1:T(2,128)S(1)} async-done(((f32[2,8,32]{2,0,1:T(2,128)}), f32[2,8,32]{2,0,1:T(2,128)S(1)}, u32[]{:S(2)}, u32[]{:S(2)}) %all-to-all-start.2) | async-done | bytes 2080 | tf_op jit(solution)/shard_map/all_to_all | solution.py:137
  108.8 3.9 %all-to-all-start.3 = ((f32[2,8,32]{2,0,1:T(2,128)}), f32[2,8,32]{2,0,1:T(2,128)S(1)}, u32[]{:S(2)}, u32[]{:S(2)}) async-start(f32[2,8,32]{2,0,1:T(2,128)} %copy.19), calls=%async_computation.3 | async-start | bytes 16384 | tf_op jit(solution)/shard_map/all_to_all | solution.py:138
  112.7 4.6 %all-to-all-done.3 = f32[2,8,32]{2,0,1:T(2,128)S(1)} async-done(((f32[2,8,32]{2,0,1:T(2,128)}), f32[2,8,32]{2,0,1:T(2,128)S(1)}, u32[]{:S(2)}, u32[]{:S(2)}) %all-to-all-start.3) | async-done | bytes 2080 | tf_op jit(solution)/shard_map/all_to_all | solution.py:138
  117.4 0.6 copy.31
  (56 shorter events, 3.9 us)
Async XLA Ops:
  0.6 20.1 %copy-start.3 = (f32[2]{0:T(128)S(1)}, f32[2]{0:T(128)}, u32[]{:S(2)}) copy-start(f32[2]{0:T(128)} %param.13) | copy-start | bytes 28
  0.6 33.8 %copy-start.1 = (f32[2,256]{1,0:T(2,128)S(1)}, f32[2,256]{1,0:T(2,128)}, u32[]{:S(2)}) copy-start(f32[2,256]{1,0:T(2,128)} %param.10) | copy-start | bytes 6148
  0.7 33.7 %copy-start.2 = (s32[2,256]{1,0:T(2,128)S(1)}, s32[2,256]{1,0:T(2,128)}, u32[]{:S(2)}) copy-start(s32[2,256]{1,0:T(2,128)} %param.11) | copy-start | bytes 6148
  0.7 33.7 %copy-start = (s32[2]{0:T(128)S(1)}, s32[2]{0:T(128)}, u32[]{:S(2)}) copy-start(s32[2]{0:T(128)} %param.12) | copy-start | bytes 28
  8.7 21.0 %all-to-all-start = ((f32[32,4,256]{2,1,0:T(4,128)}), f32[32,4,256]{2,1,0:T(4,128)S(1)}, u32[]{:S(2)}, u32[]{:S(2)}) async-start(f32[32,4,256]{2,1,0:T(4,128)} %bitcast.1), calls=%async_computation | async-start | bytes 262144 | tf_op jit(solution)/shard_map/all_to_all | solution.py:22
  30.0 4.3 %collective-permute-start = (f32[2]{0:T(128)S(1)}, f32[2]{0:T(128)S(1)}, u32[]{:S(2)}, u32[]{:S(2)}) collective-permute-start(f32[2]{0:T(128)S(1)} %slice_reduce_fusion.1), channel_id=1, source_target_pairs={{8,0},{16,8},{24,16},{32,24},{40,32},{48,40},{56,48},{64,56},{72,6... | collective-permute-start | bytes 32 | tf_op jit(solution)/shard_map/ppermute | solution.py:36
  35.9 13.9 %all-to-all-start.1 = ((f32[32,2,2]{2,1,0:T(2,128)}), f32[32,2,2]{2,1,0:T(2,128)S(1)}, u32[]{:S(2)}, u32[]{:S(2)}) async-start(f32[32,2,2]{2,1,0:T(2,128)} %broadcast_in_dim.55), calls=%async_computation.1 | async-start | bytes 65536 | tf_op jit(solution)/shard_map/all_to_all | solution.py:41
  100.6 8.2 %all-to-all-start.2 = ((f32[2,8,32]{2,0,1:T(2,128)}), f32[2,8,32]{2,0,1:T(2,128)S(1)}, u32[]{:S(2)}, u32[]{:S(2)}) async-start(f32[2,8,32]{2,0,1:T(2,128)} %copy.18), calls=%async_computation.2 | async-start | bytes 16384 | tf_op jit(solution)/shard_map/all_to_all | solution.py:137
  108.8 8.6 %all-to-all-start.3 = ((f32[2,8,32]{2,0,1:T(2,128)}), f32[2,8,32]{2,0,1:T(2,128)S(1)}, u32[]{:S(2)}, u32[]{:S(2)}) async-start(f32[2,8,32]{2,0,1:T(2,128)} %copy.19), calls=%async_computation.3 | async-start | bytes 16384 | tf_op jit(solution)/shard_map/all_to_all | solution.py:138
where the time goes:
time: 119 us
  blocking collectives  43.6 us (37%)
  waiting for transfers between devices  29.3 us (25%)
  starting transfers between devices  25.8 us (22%)
  other arithmetic  9.9 us (8%)
  local copies, waits for them, and re-layouts  5.74 us (5%)
  between operations  3.44 us (3%)
    psum x4, blocking collectives, one_axis_at_a_time(): array = lax.psum(array, axis)  43.6 us
    all_to_all x1, starting transfers between devices, sent_and_summed(): lax.all_to_all(cut_along(array, dim, devices), axis, 0, 0, tiled=True)  11.9 us
    all_to_all x1, waiting for transfers between devices, sent_and_summed(): lax.all_to_all(cut_along(array, dim, devices), axis, 0, 0, tiled=True)  8.98 us
    all_to_all x1, waiting for transfers between devices, sent_to_all(): lax.all_to_all(jnp.broadcast_to(array[None], (devices, *array.shape)), ax...  8.76 us
    reduce_sum x1, other arithmetic, per_device(): part_squares = jnp.sum(wide_rows * wide_rows, -1)  6.65 us
    all_to_all x1, starting transfers between devices, sent_to_all(): lax.all_to_all(jnp.broadcast_to(array[None], (devices, *array.shape)), ax...  5.16 us
    all_to_all x1, waiting for transfers between devices, per_device(): lax.all_to_all(returns, BATCH, split_axis=1, concat_axis=0, tiled=True)  4.64 us
    all_to_all x1, waiting for transfers between devices, per_device(): lax.all_to_all(whitened, BATCH, split_axis=1, concat_axis=0, tiled=True)  3.96 us
  transfers between devices with their start and end apart: 5, of which 5 were waited for; matrix products, arithmetic and copies ran while one was open for 1% of the time, Pallas kernels for 0%

commit v1 on v0

--- a/solution.py
+++ b/solution.py
@@ -133,9 +133,18 @@
     mean = first / count
     var = jnp.maximum(second / count - mean * mean, 1.0)
     whitened = (gae - mean) * valid * lax.rsqrt(var)
+    enter_outputs = lambda sample, shard_axis: jnp.concatenate(
+        lax.all_to_all(
+            jnp.stack(jnp.split(sample, lax.axis_size(shard_axis), 1), 0),
+            shard_axis,
+            split_axis=0,
+            concat_axis=0,
+        ),
+        0,
+    )
     out_adv, out_returns = (
         lax.all_to_all(whitened, BATCH, split_axis=1, concat_axis=0, tiled=True),
-        lax.all_to_all(returns, BATCH, split_axis=1, concat_axis=0, tiled=True),
+        enter_outputs(returns, BATCH),
     )
     return (out_adv, out_returns)
 

time: 119 us -> 120 us (level)
  starting transfers between devices: 25.8 us -> 30.7 us
  local copies, waits for them, and re-layouts: 5.74 us -> 9.98 us
  blocking collectives: 43.6 us -> 39.6 us
  waiting for transfers between devices: 29.3 us -> 25.4 us
    all_to_all x1, starting transfers between devices: 3.94 us -> 8.85 us  [per_device(): lax.all_to_all(jnp.stack(jnp.split(sample, lax.axis_size(shard_axis), 1),...]
    all_to_all x1, waiting for transfers between devices: 4.64 us -> 0.01 us  [per_device(): lax.all_to_all(jnp.stack(jnp.split(sample, lax.axis_size(shard_axis), 1),...]
    unnamed x10 -> x17, local copies, waits for them, and re-layouts: 1.21 us -> 5.5 us
    psum x4, blocking collectives: 43.6 us -> 39.6 us  [one_axis_at_a_time(): array = lax.psum(array, axis)]
  transfers between devices with their start and end apart: 5 -> 5, of which waited for: 5 -> 4; matrix products, arithmetic and copies ran while one was open for 1% -> 1% of each run, Pallas kernels for 0% -> 0%
where the time goes in v1:
time: 120 us
  blocking collectives  39.6 us (33%)
  starting transfers between devices  30.7 us (26%)
  waiting for transfers between devices  25.4 us (21%)
  local copies, waits for them, and re-layouts  9.98 us (8%)
  other arithmetic  9.97 us (8%)
  between operations  3.5 us (3%)
    psum x4, blocking collectives, one_axis_at_a_time(): array = lax.psum(array, axis)  39.6 us
    all_to_all x1, starting transfers between devices, sent_and_summed(): lax.all_to_all(cut_along(array, dim, devices), axis, 0, 0, tiled=True)  11.9 us
    all_to_all x1, waiting for transfers between devices, sent_and_summed(): lax.all_to_all(cut_along(array, dim, devices), axis, 0, 0, tiled=True)  8.98 us
    all_to_all x1, starting transfers between devices, per_device(): lax.all_to_all(jnp.stack(jnp.split(sample, lax.axis_size(shard_axis), 1),...  8.85 us
    all_to_all x1, waiting for transfers between devices, sent_to_all(): lax.all_to_all(jnp.broadcast_to(array[None], (devices, *array.shape)), ax...  8.76 us
    reduce_sum x1, other arithmetic, per_device(): part_squares = jnp.sum(wide_rows * wide_rows, -1)  6.65 us
    unnamed x17, local copies, waits for them, and re-layouts  5.5 us
    all_to_all x1, starting transfers between devices, sent_to_all(): lax.all_to_all(jnp.broadcast_to(array[None], (devices, *array.shape)), ax...  5.16 us
  transfers between devices with their start and end apart: 5, of which 4 were waited for; matrix products, arithmetic and copies ran while one was open for 1% of the time, Pallas kernels for 0%

profile of v1, /device:TPU:1, one launch (start us, length us, event | category | flops | bytes accessed | tf_op | source)
XLA Modules:
  0.0 119.8 jit_solution(16517939303517614086)
XLA Ops:
  0.7 0.7 mul.124
  1.4 6.7 %fusion = (f32[2,8192]{1,0:T(2,128)S(1)}, f32[2,8192]{1,0:T(2,128)S(1)}) fusion(bf16[2,8192,128]{2,1,0:T(8,128)(2,1)} %param.7, f32[128]{0:T(128)S(1)} %mul.124), kind=kLoop, calls=%fused_computation.2 | loop fusion | flops 10452992 | bytes 4325888 | tf_op jit(solution)/shard_map/reduce_sum | solution.py:95
  8.0 0.7 pad_maximum_fusion
  8.7 11.9 %all-to-all-start = ((f32[32,4,256]{2,1,0:T(4,128)}), f32[32,4,256]{2,1,0:T(4,128)S(1)}, u32[]{:S(2)}, u32[]{:S(2)}) async-start(f32[32,4,256]{2,1,0:T(4,128)} %bitcast.1), calls=%async_computation | async-start | bytes 262144 | tf_op jit(solution)/shard_map/all_to_all | solution.py:22
  20.8 9.0 %all-to-all-done = f32[32,4,256]{2,1,0:T(4,128)S(1)} async-done(((f32[32,4,256]{2,1,0:T(4,128)}), f32[32,4,256]{2,1,0:T(4,128)S(1)}, u32[]{:S(2)}, u32[]{:S(2)}) %all-to-all-start) | async-done | bytes 131104 | tf_op jit(solution)/shard_map/all_to_all | solution.py:22
  30.0 1.3 %collective-permute-start = (f32[2]{0:T(128)S(1)}, f32[2]{0:T(128)S(1)}, u32[]{:S(2)}, u32[]{:S(2)}) collective-permute-start(f32[2]{0:T(128)S(1)} %slice_reduce_fusion.1), channel_id=1, source_target_pairs={{8,0},{16,8},{24,16},{32,24},{40,32},{48,40},{56,48},{64,56},{72,6... | collective-permute-start | bytes 32 | tf_op jit(solution)/shard_map/ppermute | solution.py:36
  31.3 3.0 %collective-permute-done = f32[2]{0:T(128)S(1)} collective-permute-done((f32[2]{0:T(128)S(1)}, f32[2]{0:T(128)S(1)}, u32[]{:S(2)}, u32[]{:S(2)}) %collective-permute-start) | collective-permute-done | bytes 40 | tf_op jit(solution)/shard_map/ppermute | solution.py:36
  34.5 0.7 fusion.2
  35.9 5.2 %all-to-all-start.1 = ((f32[32,2,2]{2,1,0:T(2,128)}), f32[32,2,2]{2,1,0:T(2,128)S(1)}, u32[]{:S(2)}, u32[]{:S(2)}) async-start(f32[32,2,2]{2,1,0:T(2,128)} %broadcast_in_dim.55), calls=%async_computation.1 | async-start | bytes 65536 | tf_op jit(solution)/shard_map/all_to_all | solution.py:41
  41.1 8.8 %all-to-all-done.1 = f32[32,2,2]{2,1,0:T(2,128)S(1)} async-done(((f32[32,2,2]{2,1,0:T(2,128)}), f32[32,2,2]{2,1,0:T(2,128)S(1)}, u32[]{:S(2)}, u32[]{:S(2)}) %all-to-all-start.1) | async-done | bytes 544 | tf_op jit(solution)/shard_map/all_to_all | solution.py:41
  52.3 0.7 compare_select_fusion
  53.5 0.6 constant_dynamic-update-slice_fusion.6
  54.2 0.6 constant_dynamic-update-slice_fusion.5
  54.8 0.6 constant_dynamic-update-slice_fusion.4
  56.0 0.6 constant_dynamic-update-slice_fusion.2
  56.6 0.6 constant_dynamic-update-slice_fusion.1
  57.9 8.9 %all-to-all-start.3 = ((f32[8,2,32]{2,1,0:T(2,128)}), f32[8,2,32]{2,1,0:T(2,128)S(1)}, u32[]{:S(2)}, u32[]{:S(2)}) async-start(f32[8,2,32]{2,1,0:T(2,128)} %constant_dynamic-update-slice_fusion), calls=%async_computation.3 | async-start | bytes 16384 | tf_op jit(solution)/shard_map/all_to_all | solution.py:137
  66.7 0.7 fusion.20
  67.4 7.6 %all-reduce.2 = (f32[]{:T(128)}, f32[]{:T(128)}, f32[]{:T(128)}) all-reduce(f32[]{:T(128)} %get-tuple-element.5, f32[]{:T(128)} %get-tuple-element.24, f32[]{:T(128)} %get-tuple-element.4), channel_id=1, replica_groups=mesh['seq_0'=4,'seq_1'=8,'batch_0'=4,'batch_1'=2] {'seq_0'}, use_global_device_ids=true, to_apply=%region_14.15 | all-reduce | flops 3 | bytes 24 | tf_op jit(solution)/shard_map/psum | solution.py:87
  75.0 11.8 %all-reduce = (f32[]{:T(128)}, f32[]{:T(128)}, f32[]{:T(128)}) all-reduce(f32[]{:T(128)} %get-tuple-element.12, f32[]{:T(128)} %get-tuple-element.13, f32[]{:T(128)} %get-tuple-element.14), channel_id=1, replica_groups=mesh['seq_0'=4,'seq_1'=8,'batch_0'=4,'batch_1'=2] {'seq_1'}, use_global_device_ids=true, to_apply=%region_15.16 | all-reduce | flops 3 | bytes 24 | tf_op jit(solution)/shard_map/psum | solution.py:87
  86.7 9.3 %all-reduce.1 = (f32[]{:T(128)}, f32[]{:T(128)}, f32[]{:T(128)}) all-reduce(f32[]{:T(128)} %get-tuple-element.6, f32[]{:T(128)} %get-tuple-element.7, f32[]{:T(128)} %get-tuple-element.8), channel_id=1, replica_groups=mesh['seq_0'=4,'seq_1'=8,'batch_0'=4,'batch_1'=2] {'batch_0'}, use_global_device_ids=true, to_apply=%region_16.17 | all-reduce | flops 3 | bytes 24 | tf_op jit(solution)/shard_map/psum | solution.py:87
  96.1 10.9 %all-reduce.3 = (f32[]{:T(128)}, f32[]{:T(128)}, f32[]{:T(128)}) all-reduce(f32[]{:T(128)} %get-tuple-element.9, f32[]{:T(128)} %get-tuple-element.10, f32[]{:T(128)} %get-tuple-element.11), channel_id=1, replica_groups=mesh['seq_0'=4,'seq_1'=8,'batch_0'=4,'batch_1'=2] {'batch_1'}, use_global_device_ids=true, to_apply=%region_17.18 | all-reduce | flops 3 | bytes 24 | tf_op jit(solution)/shard_map/psum | solution.py:87
  110.4 3.6 %all-to-all-start.2 = ((f32[2,8,32]{2,0,1:T(2,128)}), f32[2,8,32]{2,0,1:T(2,128)S(1)}, u32[]{:S(2)}, u32[]{:S(2)}) async-start(f32[2,8,32]{2,0,1:T(2,128)} %copy.16), calls=%async_computation.2 | async-start | bytes 16384 | tf_op jit(solution)/shard_map/all_to_all | solution.py:146
  114.0 4.6 %all-to-all-done.2 = f32[2,8,32]{2,0,1:T(2,128)S(1)} async-done(((f32[2,8,32]{2,0,1:T(2,128)}), f32[2,8,32]{2,0,1:T(2,128)S(1)}, u32[]{:S(2)}, u32[]{:S(2)}) %all-to-all-start.2) | async-done | bytes 2080 | tf_op jit(solution)/shard_map/all_to_all | solution.py:146
  (62 shorter events, 7.4 us)
Async XLA Ops:
  0.6 20.1 %copy-start.3 = (f32[2]{0:T(128)S(1)}, f32[2]{0:T(128)}, u32[]{:S(2)}) copy-start(f32[2]{0:T(128)} %param.13) | copy-start | bytes 28
  0.6 33.8 %copy-start.1 = (f32[2,256]{1,0:T(2,128)S(1)}, f32[2,256]{1,0:T(2,128)}, u32[]{:S(2)}) copy-start(f32[2,256]{1,0:T(2,128)} %param.10) | copy-start | bytes 6148
  0.7 33.7 %copy-start.2 = (s32[2,256]{1,0:T(2,128)S(1)}, s32[2,256]{1,0:T(2,128)}, u32[]{:S(2)}) copy-start(s32[2,256]{1,0:T(2,128)} %param.11) | copy-start | bytes 6148
  0.7 33.7 %copy-start = (s32[2]{0:T(128)S(1)}, s32[2]{0:T(128)}, u32[]{:S(2)}) copy-start(s32[2]{0:T(128)} %param.12) | copy-start | bytes 28
  8.7 21.0 %all-to-all-start = ((f32[32,4,256]{2,1,0:T(4,128)}), f32[32,4,256]{2,1,0:T(4,128)S(1)}, u32[]{:S(2)}, u32[]{:S(2)}) async-start(f32[32,4,256]{2,1,0:T(4,128)} %bitcast.1), calls=%async_computation | async-start | bytes 262144 | tf_op jit(solution)/shard_map/all_to_all | solution.py:22
  30.0 4.3 %collective-permute-start = (f32[2]{0:T(128)S(1)}, f32[2]{0:T(128)S(1)}, u32[]{:S(2)}, u32[]{:S(2)}) collective-permute-start(f32[2]{0:T(128)S(1)} %slice_reduce_fusion.1), channel_id=1, source_target_pairs={{8,0},{16,8},{24,16},{32,24},{40,32},{48,40},{56,48},{64,56},{72,6... | collective-permute-start | bytes 32 | tf_op jit(solution)/shard_map/ppermute | solution.py:36
  35.9 13.9 %all-to-all-start.1 = ((f32[32,2,2]{2,1,0:T(2,128)}), f32[32,2,2]{2,1,0:T(2,128)S(1)}, u32[]{:S(2)}, u32[]{:S(2)}) async-start(f32[32,2,2]{2,1,0:T(2,128)} %broadcast_in_dim.55), calls=%async_computation.1 | async-start | bytes 65536 | tf_op jit(solution)/shard_map/all_to_all | solution.py:41
  57.9 52.5 %all-to-all-start.3 = ((f32[8,2,32]{2,1,0:T(2,128)}), f32[8,2,32]{2,1,0:T(2,128)S(1)}, u32[]{:S(2)}, u32[]{:S(2)}) async-start(f32[8,2,32]{2,1,0:T(2,128)} %constant_dynamic-update-slice_fusion), calls=%async_computation.3 | async-start | bytes 16384 | tf_op jit(solution)/shard_map/all_to_all | solution.py:137
  110.4 8.2 %all-to-all-start.2 = ((f32[2,8,32]{2,0,1:T(2,128)}), f32[2,8,32]{2,0,1:T(2,128)S(1)}, u32[]{:S(2)}, u32[]{:S(2)}) async-start(f32[2,8,32]{2,0,1:T(2,128)} %copy.16), calls=%async_computation.2 | async-start | bytes 16384 | tf_op jit(solution)/shard_map/all_to_all | solution.py:146
